TPU v7x, 32 devices: a whole 2x2x4 slice. The times are simulated.
32 devices in a mesh: expert: 8 (over z, y), replica: 2 (over core), group: 2 (over x).
Axes of the slice: x: 2, y: 2, z: 4, core: 2. Of those that a mesh axis runs over, the one named last changes fastest.
Arguments:
- tokens: bfloat16 [1536, 4096], P('expert', 'group'), may hold values from -6 to 6
- expert_ids: int32 [1536, 8], P('expert'), may hold values from 0 to 127, all different within a row; in each aligned block of 192 rows (0 to 191, 192 to 383, ...) at most 15 rows name the same one
- route_gates: float32 [1536, 8], P('expert'), may hold values from 0.03 to 0.5
- member_order: int32 [8], replicated, may hold values from 0 to 7, each once
- teach_gate: bfloat16 [8, 1536, 4096], P('expert', 'replica', 'group'), may hold values from -0.09375 to 0.09375
- teach_up: bfloat16 [8, 1536, 4096], P('expert', 'replica', 'group'), may hold values from -0.09375 to 0.09375
- teach_down: bfloat16 [8, 1536, 4096], P('expert', 'replica', 'group'), may hold values from -0.15625 to 0.15625
- stud_gate: bfloat16 [8, 1536, 2048], P('expert', 'replica', 'group'), may hold values from -0.09375 to 0.09375
- stud_up: bfloat16 [8, 1536, 2048], P('expert', 'replica', 'group'), may hold values from -0.09375 to 0.09375
- stud_down: bfloat16 [8, 1536, 2048], P('expert', 'replica', 'group'), may hold values from -0.15625 to 0.15625
Outputs:
- residual: float32 [1536, 4096], P('expert', ('group', 'replica'))
- grad_gate: bfloat16 [8, 1536, 2048], P('expert', 'replica', 'group')
- grad_up: bfloat16 [8, 1536, 2048], P('expert', 'replica', 'group')
- grad_down: bfloat16 [8, 1536, 2048], P('expert', 'replica', 'group')
Inputs may be any that keep to these rules, and one draw needn't show every extreme that they name: `expert_ids`: each row names 8 different experts. Within each aligned block of 192 rows no expert is named by more than 15 rows. Only experts below 8 are in the window. `member_order`: every teacher expert of the window appears once.
All inputs are finite; a program needn't handle non-finite values.
Results may differ from a plain program's by a relative error of at most 0.025.
Values may be sent and summed in bfloat16 or wider, within the bound.
No kernel may reach another device: no remote copies, remote signals or barrier semaphores. Data moves between devices by JAX's collectives and lax.ppermute only.
A program may use at most 128 MiB of HBM per device.

v0:
```python
import jax
import jax.numpy as jnp
from jax import lax
from jax.sharding import PartitionSpec as P

CAP = 15


def from_partner(block, axis, bit):
    count = lax.axis_size(axis)
    route = []
    for low in range(count):
        high = low | 1 << bit
        if high != low and high < count:
            route += [(low, high), (high, low)]
    return lax.ppermute(block, axis, route)


def matmul(left_side, right_side):
    return jnp.dot(left_side, right_side, preferred_element_type=jnp.float32)


def across_width(left_side, right_side):
    return lax.dot_general(
        left_side, right_side, (((1,), (1,)), ((), ())), preferred_element_type=jnp.float32
    )


def inner_rows(left_side, right_side):
    return lax.dot_general(
        left_side, right_side, (((0,), (0,)), ((), ())), preferred_element_type=jnp.float32
    )


def slot_tables(expert_ids, route_gates, experts_here, capacity):
    tok_count, top_count = expert_ids.shape
    pair_count = tok_count * top_count
    flat_ids = expert_ids.reshape(pair_count)
    flat_gates = route_gates.reshape(pair_count)
    inside = flat_ids < experts_here
    columns = lax.broadcasted_iota(jnp.int32, (pair_count, experts_here), 1)
    onehot = (flat_ids[:, None] == columns).astype(jnp.int32)
    rank_rows = jnp.sum(onehot * (jnp.cumsum(onehot, axis=0) - 1), axis=1)
    target = jnp.where(inside, flat_ids * capacity + rank_rows, experts_here * capacity)
    slot_table = jnp.full((experts_here * capacity,), pair_count, jnp.int32)
    slot_table = slot_table.at[target].set(jnp.arange(pair_count, dtype=jnp.int32), mode="drop")
    filled = slot_table < pair_count
    clamped = jnp.minimum(slot_table, pair_count - 1)
    token_row = clamped // top_count
    weights = jnp.where(filled, flat_gates[clamped], jnp.zeros((), jnp.float32))
    return (token_row, filled, weights)


def arrange_student(returned, inverse, capacity, columns, narrow):
    owners = returned.shape[0]
    shaped = returned.reshape(owners // 2, 2, 2, capacity, columns, narrow)
    by_place = shaped.transpose(0, 2, 3, 4, 1, 5).reshape(owners, capacity, columns * 2 * narrow)
    return by_place[inverse].reshape(owners * capacity, columns * 2 * narrow).astype(jnp.float32)


def shards(
    tokens,
    expert_ids,
    route_gates,
    member_order,
    teach_gate,
    teach_up,
    teach_down,
    stud_gate,
    stud_up,
    stud_down,
):
    owners = lax.axis_size("expert")
    replicas = lax.axis_size("replica")
    tok_count, half_width = tokens.shape
    block_width = half_width // replicas
    narrow = block_width // 2
    capacity = CAP
    token_row, filled, weights = slot_tables(expert_ids, route_gates, owners, capacity)
    picked = jnp.where(filled[:, None], tokens[token_row], jnp.zeros((), jnp.bfloat16))
    teach_send = picked.reshape(owners, capacity, half_width)
    dest_pairs = jnp.repeat(member_order.reshape(owners // 2, 2), 2, axis=0)
    members = teach_send[dest_pairs].reshape(owners, 2 * capacity, replicas, 2, narrow)
    parity = (jnp.arange(owners) % 2)[:, None, None, None]
    stud_send = jnp.where(parity == 0, members[:, :, :, 0, :], members[:, :, :, 1, :])
    stud_send = stud_send.reshape(owners, 2 * capacity, replicas * narrow)
    teach_rows, stud_rows = (
        lax.all_to_all(teach_send, "expert", split_axis=0, concat_axis=0, tiled=True),
        lax.all_to_all(stud_send, "expert", split_axis=0, concat_axis=0, tiled=True),
    )
    teach_in = teach_rows.reshape(owners * capacity, half_width)
    stud_in = stud_rows.reshape(owners * 2 * capacity, replicas * narrow)
    teach_stack = jnp.stack(
        [across_width(teach_in, teach_gate[0]), across_width(teach_in, teach_up[0])]
    )
    teach_stack = lax.psum(teach_stack.astype(jnp.bfloat16), "group").astype(jnp.float32)
    teach_hidden = (teach_stack[0] * jax.nn.sigmoid(teach_stack[0]) * teach_stack[1]).astype(
        jnp.bfloat16
    )
    teach_part = matmul(teach_hidden, teach_down[0])
    stud_stack = jnp.stack([across_width(stud_in, stud_gate[0]), across_width(stud_in, stud_up[0])])
    stud_stack = lax.psum(stud_stack.astype(jnp.bfloat16), "group").astype(jnp.float32)
    stud_stack = stud_stack + from_partner(stud_stack.astype(jnp.bfloat16), "expert", 0).astype(
        stud_stack.dtype
    )
    gate_pre = stud_stack[0]
    up_pre = stud_stack[1]
    sigmoid_gate = jax.nn.sigmoid(gate_pre)
    stud_hidden = (gate_pre * sigmoid_gate * up_pre).astype(jnp.bfloat16)
    stud_part = matmul(stud_hidden, stud_down[0])
    inverse = (
        jnp.zeros((owners,), jnp.int32).at[member_order].set(jnp.arange(owners, dtype=jnp.int32))
    )
    slot_rows = lax.broadcasted_iota(jnp.int32, (tok_count, owners * capacity), 0)
    token_onehot = ((token_row[None, :] == slot_rows) & filled[None, :]).astype(jnp.float32)
    teach_back, stud_back = (
        lax.all_to_all(
            teach_part.astype(jnp.bfloat16).reshape(owners, capacity, half_width),
            "expert",
            split_axis=0,
            concat_axis=0,
            tiled=True,
        ),
        lax.all_to_all(
            stud_part.astype(jnp.bfloat16).reshape(owners, 2 * capacity, replicas * narrow),
            "expert",
            split_axis=0,
            concat_axis=0,
            tiled=True,
        ),
    )
    teach_out = teach_back.reshape(owners * capacity, half_width).astype(jnp.float32)
    stud_out = arrange_student(stud_back, inverse, capacity, replicas, narrow)
    term_rows = weights[:, None] * (stud_out - teach_out)
    spread = jnp.dot(
        token_onehot, term_rows, precision=lax.Precision.HIGHEST, preferred_element_type=jnp.float32
    )
    residual = lax.psum_scatter(
        spread.reshape(tok_count, replicas, block_width).astype(jnp.bfloat16),
        "replica",
        scatter_dimension=1,
        tiled=True,
    ).astype(jnp.float32)
    residual = residual.reshape(tok_count, block_width)
    grad_slots = (weights[:, None] * residual[token_row]).astype(jnp.bfloat16)
    grad_slots = grad_slots.reshape(owners, capacity, 2, narrow)[member_order]
    grad_send = grad_slots.reshape(owners // 2, 2, capacity, 2, narrow).transpose(0, 3, 1, 2, 4)
    grad_send = grad_send.reshape(owners, 2 * capacity, narrow)
    grad_in = lax.all_to_all(grad_send, "expert", split_axis=0, concat_axis=0, tiled=True).reshape(
        owners * 2 * capacity, narrow
    )
    down_local = stud_down[0]
    column_piece = lax.all_gather(grad_in, "replica", axis=1, tiled=True)
    back_hidden = across_width(column_piece, down_local)
    down_grad = inner_rows(stud_hidden, column_piece)
    back_hidden, down_grad = (back_hidden, down_grad)
    back_hidden = lax.psum(back_hidden.astype(jnp.bfloat16), "group").astype(jnp.float32)
    back_hidden = back_hidden + from_partner(back_hidden.astype(jnp.bfloat16), "expert", 0).astype(
        back_hidden.dtype
    )
    gate_rows = (
        back_hidden * up_pre * sigmoid_gate * (1.0 + gate_pre * (1.0 - sigmoid_gate))
    ).astype(jnp.bfloat16)
    up_rows = (back_hidden * gate_pre * sigmoid_gate).astype(jnp.bfloat16)
    grad_gate = inner_rows(gate_rows, stud_in).astype(jnp.bfloat16)[None]
    grad_up = inner_rows(up_rows, stud_in).astype(jnp.bfloat16)[None]
    grad_down = down_grad.astype(jnp.bfloat16)[None]
    return (residual, grad_gate, grad_up, grad_down)


def solution(mesh):
    placed = (
        P("expert", "group"),
        P("expert", None),
        P("expert", None),
        P(),
        P("expert", "replica", "group"),
        P("expert", "replica", "group"),
        P("expert", "replica", "group"),
        P("expert", "replica", "group"),
        P("expert", "replica", "group"),
        P("expert", "replica", "group"),
    )
    return jax.shard_map(
        shards,
        mesh=mesh,
        in_specs=placed,
        out_specs=(
            P("expert", ("group", "replica")),
            P("expert", "replica", "group"),
            P("expert", "replica", "group"),
            P("expert", "replica", "group"),
        ),
        check_vma=False,
    )
```

profile of v0, /device:TPU:0, one launch (start us, length us, event | category | flops | bytes accessed | tf_op | source)
XLA Modules:
  0.0 277.0 jit_solution(4110919144264187145)
XLA Ops:
  7.2 0.9 broadcast_compare_fusion
  8.0 0.8 broadcast_multiply_fusion.1
  8.8 0.8 copy.50
  10.4 2.3 reduce-window.6
  13.3 6.2 %scatter_custom_fusion = s32[120]{0:T(128)S(1)} fusion(s32[1536]{0:T(1024)S(1)} %fusion.81, s32[1536]{0:T(1024)S(1)} %iota.27, s32[]{:T(128)} %constant.21.clone.1), kind=kCustom, calls=%fused_computation.115 | custom fusion | bytes 484 | tf_op jit(solution)/shard_map/scatter | solution.py:46
  19.5 3.4 %gather_fusion.1 = bf16[120,2048]{1,0:T(8,128)(2,1)} fusion(bf16[192,2048]{1,0:T(8,128)(2,1)} %param.10, s32[1024]{0:T(1024)S(1)} %get-tuple-element.11), kind=kCustom, calls=%fused_computation.1 | custom fusion | bytes 983520 | tf_op jit(solution)/shard_map/gather | solution.py:80
  22.9 2.0 gather.24
  25.0 1.9 broadcast_select_fusion
  26.9 7.3 %all-to-all-start.2 = ((bf16[8,15,2048]{2,1,0:T(8,128)(2,1)}), bf16[8,15,2048]{2,1,0:T(8,128)(2,1)}, u32[]{:S(2)}, u32[]{:S(2)}) async-start(bf16[8,15,2048]{2,1,0:T(8,128)(2,1)} %broadcast_select_fusion), calls=%async_computation.2 | async-start | bytes 1048576 | tf_op jit(solution)/shard_map/all_to_all | solution.py:88
  34.8 2.6 gather_fusion.2
  37.4 3.7 %reshape.185 = bf16[8,30,2,2,512]{4,3,2,1,0:T(2,128)(2,1)} reshape(bf16[16,15,2048]{2,1,0:T(8,128)(2,1)} %gather_fusion.2) | data formatting | bytes 1966080 | tf_op jit(solution)/shard_map/reshape | solution.py:83
  41.1 7.5 %slice_reduce_fusion.1 = (bf16[8,30,2,512]{3,2,1,0:T(2,128)(2,1)}, bf16[8,30,2,512]{3,2,1,0:T(2,128)(2,1)}) fusion(bf16[8,30,2,2,512]{4,3,2,1,0:T(2,128)(2,1)} %reshape.185), kind=kLoop, calls=%fused_computation.45 | loop fusion | bytes 1966080 | tf_op jit(solution)/shard_map/slice | solution.py:85
  48.6 2.1 reshape.273
  50.7 2.1 reshape.272
  52.8 1.7 copy_select_fusion
  54.5 1.1 copy.57
  55.6 6.0 %all-to-all-start = ((bf16[8,30,1024]{2,1,0:T(8,128)(2,1)}), bf16[8,30,1024]{2,1,0:T(8,128)(2,1)}, u32[]{:S(2)}, u32[]{:S(2)}) async-start(bf16[8,30,1024]{2,1,0:T(8,128)(2,1)} %copy.57), calls=%async_computation | async-start | bytes 1048576 | tf_op jit(solution)/shard_map/all_to_all | solution.py:89
  61.8 2.0 reshape.190
  63.8 3.3 %fusion.44 = bf16[1,120,768]{2,1,0:T(8,128)(2,1)S(1)} fusion(bf16[120,2048]{1,0:T(8,128)(2,1)} %reshape.190, bf16[1,768,2048]{2,1,0:T(8,128)(2,1)} %param.15), kind=kOutput, calls=%fused_computation.39 | convolution fusion | flops 377579520 | bytes 3821568 | tf_op jit(solution)/shard_map/dot_general | solution.py:24
  67.2 1.2 fusion.47
  68.4 7.3 %all-to-all-done = bf16[8,30,1024]{2,1,0:T(8,128)(2,1)} async-done(((bf16[8,30,1024]{2,1,0:T(8,128)(2,1)}), bf16[8,30,1024]{2,1,0:T(8,128)(2,1)}, u32[]{:S(2)}, u32[]{:S(2)}) %all-to-all-start) | async-done | bytes 491552 | tf_op jit(solution)/shard_map/all_to_all | solution.py:89
  75.7 2.0 reshape.186
  77.6 2.3 fusion.32
  80.6 0.8 pad_maximum_fusion.1
  81.4 0.9 pad_maximum_fusion
  82.3 40.6 %all-reduce.6.cloned.1.call-done = (bf16[2,120,768]{2,1,0:T(8,128)(2,1)}, bf16[2,240,768]{2,1,0:T(8,128)(2,1)}) async-done(((bf16[2,120,768]{2,1,0:T(8,128)(2,1)}, bf16[2,240,768]{2,1,0:T(8,128)(2,1)}), (bf16[2,120,768]{2,1,0:T(8,128)(2,1)}, bf16[2,240,768]{2,1,0:T(8,128)(2,1)})) %all-reduce.6.cloned.1.call-update) | async-done | bytes 1105936 | tf_op jit(solution)/shard_map/psum | solution.py:96
  122.9 1.5 collective-permute-start
  124.4 16.8 %collective-permute-done = bf16[2,240,768]{2,1,0:T(8,128)(2,1)S(1)} collective-permute-done((bf16[2,240,768]{2,1,0:T(8,128)(2,1)}, bf16[2,240,768]{2,1,0:T(8,128)(2,1)S(1)}, u32[]{:S(2)}, u32[]{:S(2)}) %collective-permute-start) | collective-permute-done | bytes 737312 | tf_op jit(solution)/shard_map/ppermute | solution.py:16
  141.2 1.3 convert_add_fusion
  142.5 1.1 copy-done.3
  143.6 1.4 fusion.20
  145.0 2.0 reshape.187
  147.0 5.5 %all-to-all-start.1 = ((bf16[8,30,1024]{2,1,0:T(8,128)(2,1)}), bf16[8,30,1024]{2,1,0:T(8,128)(2,1)}, u32[]{:S(2)}, u32[]{:S(2)}) async-start(bf16[8,30,1024]{2,1,0:T(8,128)(2,1)} %reshape.187), calls=%async_computation.1 | async-start | bytes 1048576 | tf_op jit(solution)/shard_map/all_to_all | solution.py:124
  152.6 1.4 fusion.6
  153.9 2.0 reshape.191
  155.9 10.1 %all-to-all-done.1 = bf16[8,30,1024]{2,1,0:T(8,128)(2,1)} async-done(((bf16[8,30,1024]{2,1,0:T(8,128)(2,1)}), bf16[8,30,1024]{2,1,0:T(8,128)(2,1)}, u32[]{:S(2)}, u32[]{:S(2)}) %all-to-all-start.1) | async-done | bytes 491552 | tf_op jit(solution)/shard_map/all_to_all | solution.py:124
  166.1 4.2 %all-to-all-start.3 = ((bf16[8,15,2048]{2,1,0:T(8,128)(2,1)}), bf16[8,15,2048]{2,1,0:T(8,128)(2,1)}, u32[]{:S(2)}, u32[]{:S(2)}) async-start(bf16[8,15,2048]{2,1,0:T(8,128)(2,1)} %reshape.191), calls=%async_computation.3 | async-start | bytes 1048576 | tf_op jit(solution)/shard_map/all_to_all | solution.py:117
  171.1 1.1 gather_fusion
  172.3 2.1 reshape.274
  174.4 2.2 copy.68
  176.6 2.1 reshape.275
  178.7 2.4 gather_fusion.3
  181.1 2.4 all-to-all-done.3
  183.6 2.3 convert_subtract_fusion
  185.9 2.3 sub.28
  188.2 1.3 broadcast_multiply_fusion
  189.5 1.7 convolution_convert_fusion.3
  191.4 6.5 %reduce-scatter.2.cloned.1.call-done = bf16[192,1,1024]{2,0,1:T(8,128)(2,1)} async-done(((bf16[192,2,1024]{2,0,1:T(8,128)(2,1)}), bf16[192,1,1024]{2,0,1:T(8,128)(2,1)}) %reduce-scatter.2.cloned.1.call-update) | async-done | bytes 393232 | tf_op jit(solution)/shard_map/reduce_scatter | solution.py:138
  197.9 2.0 bitcast_convert_fusion
  199.9 2.9 %gather_fusion.4 = f32[120,1024]{1,0:T(8,128)} fusion(f32[192,1024]{1,0:T(8,128)} %bitcast_convert_fusion, s32[1024]{0:T(1024)S(1)} %get-tuple-element.11), kind=kCustom, calls=%fused_computation.4 | custom fusion | bytes 983520 | tf_op jit(solution)/shard_map/gather | solution.py:145
  202.8 2.2 gather.28
  205.0 1.3 multiply_convert_fusion.1
  206.3 1.7 gather_fusion.5
  208.0 1.0 copy.69
  209.7 15.2 %all_to_all.25 = bf16[8,30,512]{2,1,0:T(8,128)(2,1)S(1)} all-to-all(bf16[8,30,512]{2,1,0:T(8,128)(2,1)} %reshape.276), channel_id=1, replica_groups=mesh['expert'=8,'replica'=2,'group'=2] {'expert'}, dimensions={0} | all-to-all | bytes 491520 | tf_op jit(solution)/shard_map/all_to_all | solution.py:149
  225.6 2.6 all_gather.3
  228.2 0.8 copy-done.7
  229.0 2.8 fusion.29
  231.8 24.4 %all-reduce.4.cloned.1.call-done = bf16[240,768]{1,0:T(8,128)(2,1)} async-done(((bf16[240,768]{1,0:T(8,128)(2,1)}), bf16[240,768]{1,0:T(8,128)(2,1)}) %all-reduce.4.cloned.1.call-update) | async-done | bytes 368656 | tf_op jit(solution)/shard_map/psum | solution.py:157
  256.2 1.5 collective-permute-start.1
  257.6 3.3 %fusion.19 = bf16[1,768,1024]{2,1,0:T(8,128)(2,1)} fusion(bf16[240,1024]{1,0:T(8,128)(2,1)} %copy-done.7, f32[2,240,768]{2,1,0:T(8,128)} %copy-done.3), kind=kOutput, calls=%fused_computation.28 | convolution fusion | flops 379379712 | bytes 3538944 | tf_op jit(solution)/shard_map/dot_general | solution.py:30
  260.9 5.7 %collective-permute-done.1 = bf16[240,768]{1,0:T(8,128)(2,1)S(1)} collective-permute-done((bf16[240,768]{1,0:T(8,128)(2,1)}, bf16[240,768]{1,0:T(8,128)(2,1)S(1)}, u32[]{:S(2)}, u32[]{:S(2)}) %collective-permute-start.1) | collective-permute-done | bytes 368672 | tf_op jit(solution)/shard_map/ppermute | solution.py:16
  266.6 2.0 fusion.17
  268.6 1.9 fusion.18
  (73 shorter events, 5.5 us)
Async XLA Ops:
  7.2 145.4 %copy-start = (bf16[1,768,2048]{2,1,0:T(8,128)(2,1)S(1)}, bf16[1,768,2048]{2,1,0:T(8,128)(2,1)}, u32[]{:S(2)}) copy-start(bf16[1,768,2048]{2,1,0:T(8,128)(2,1)} %param.16) | copy-start | bytes 9437188
  22.9 11.3 %copy-start.10 = (s32[8]{0:T(128)S(1)}, s32[8]{0:T(128)}, u32[]{:S(2)}) copy-start(s32[8]{0:T(128)} %param.13) | copy-start | bytes 100
  26.9 28.7 %all-to-all-start.2 = ((bf16[8,15,2048]{2,1,0:T(8,128)(2,1)}), bf16[8,15,2048]{2,1,0:T(8,128)(2,1)}, u32[]{:S(2)}, u32[]{:S(2)}) async-start(bf16[8,15,2048]{2,1,0:T(8,128)(2,1)} %broadcast_select_fusion), calls=%async_computation.2 | async-start | bytes 1048576 | tf_op jit(solution)/shard_map/all_to_all | solution.py:88
  55.6 20.1 %all-to-all-start = ((bf16[8,30,1024]{2,1,0:T(8,128)(2,1)}), bf16[8,30,1024]{2,1,0:T(8,128)(2,1)}, u32[]{:S(2)}, u32[]{:S(2)}) async-start(bf16[8,30,1024]{2,1,0:T(8,128)(2,1)} %copy.57), calls=%async_computation | async-start | bytes 1048576 | tf_op jit(solution)/shard_map/all_to_all | solution.py:89
  61.6 61.3 %all-reduce.6.cloned.1.call-start = ((), (), s32[]{:S(2)}) async-start(), calls=%async_computation.8 | async-start | bytes 2211840 | tf_op jit(solution)/shard_map/psum | solution.py:96
  63.8 3.4 %copy-start.1 = (bf16[120,2048]{1,0:T(8,128)(2,1)S(1)}, bf16[120,2048]{1,0:T(8,128)(2,1)}, u32[]{:S(2)}) copy-start(bf16[120,2048]{1,0:T(8,128)(2,1)} %reshape.190) | copy-start | bytes 1474564
  63.8 3.4 %copy-start.2 = (bf16[1,768,2048]{2,1,0:T(8,128)(2,1)S(1)}, bf16[1,768,2048]{2,1,0:T(8,128)(2,1)}, u32[]{:S(2)}) copy-start(bf16[1,768,2048]{2,1,0:T(8,128)(2,1)} %param.14) | copy-start | bytes 9437188
  77.6 2.3 copy-start.5
  77.6 2.3 copy-start.11
  122.9 20.7 %copy-start.12 = (bf16[1,768,1024]{2,1,0:T(8,128)(2,1)S(1)}, bf16[1,768,1024]{2,1,0:T(8,128)(2,1)}, u32[]{:S(2)}) copy-start(bf16[1,768,1024]{2,1,0:T(8,128)(2,1)} %param.19) | copy-start | bytes 4718596
  122.9 18.3 %collective-permute-start = (bf16[2,240,768]{2,1,0:T(8,128)(2,1)}, bf16[2,240,768]{2,1,0:T(8,128)(2,1)S(1)}, u32[]{:S(2)}, u32[]{:S(2)}) collective-permute-start(bf16[2,240,768]{2,1,0:T(8,128)(2,1)} %get-tuple-element.7), channel_id=1, source_target_pairs={{0,4},{4,0},{8,12},{12,8},{16,20},{20,16},{24,28},{28,24},{1,5},{5... | collective-permute-start | bytes 2211848 | tf_op jit(solution)/shard_map/ppermute | solution.py:16
  142.5 1.1 copy-start.3
  145.0 7.5 %copy-start.8 = (bf16[2,120,768]{2,1,0:T(8,128)(2,1)S(1)}, bf16[2,120,768]{2,1,0:T(8,128)(2,1)}, u32[]{:S(2)}) copy-start(bf16[2,120,768]{2,1,0:T(8,128)(2,1)} %get-tuple-element.6) | copy-start | bytes 1105924
  147.0 19.1 %all-to-all-start.1 = ((bf16[8,30,1024]{2,1,0:T(8,128)(2,1)}), bf16[8,30,1024]{2,1,0:T(8,128)(2,1)}, u32[]{:S(2)}, u32[]{:S(2)}) async-start(bf16[8,30,1024]{2,1,0:T(8,128)(2,1)} %reshape.187), calls=%async_computation.1 | async-start | bytes 1048576 | tf_op jit(solution)/shard_map/all_to_all | solution.py:124
  153.9 16.3 %copy-start.9 = (f32[192,8]{0,1:T(8,128)S(1)}, f32[192,8]{0,1:T(8,128)}, u32[]{:S(2)}) copy-start(f32[192,8]{0,1:T(8,128)} %param.12) | copy-start | bytes 18436
  166.1 17.5 %all-to-all-start.3 = ((bf16[8,15,2048]{2,1,0:T(8,128)(2,1)}), bf16[8,15,2048]{2,1,0:T(8,128)(2,1)}, u32[]{:S(2)}, u32[]{:S(2)}) async-start(bf16[8,15,2048]{2,1,0:T(8,128)(2,1)} %reshape.191), calls=%async_computation.3 | async-start | bytes 1048576 | tf_op jit(solution)/shard_map/all_to_all | solution.py:117
  170.2 27.7 %reduce-scatter.2.cloned.1.call-start = ((), (), s32[]{:S(2)}) async-start(), calls=%async_computation.6 | async-start | bytes 1179648 | tf_op jit(solution)/shard_map/reduce_scatter | solution.py:138
  191.2 64.9 %all-reduce.4.cloned.1.call-start = ((), (), s32[]{:S(2)}) async-start(), calls=%async_computation.7 | async-start | bytes 737280 | tf_op jit(solution)/shard_map/psum | solution.py:157
  228.2 0.8 copy-start.7
  256.2 10.4 %copy-start.4 = (f32[2,240,768]{2,1,0:T(8,128)S(1)}, f32[2,240,768]{2,1,0:T(8,128)}, u32[]{:S(2)}) copy-start(f32[2,240,768]{2,1,0:T(8,128)} %copy-done.3) | copy-start | bytes 4423684
  256.2 10.4 %copy-start.6 = (bf16[240,1024]{1,0:T(8,128)(2,1)S(1)}, bf16[240,1024]{1,0:T(8,128)(2,1)}, u32[]{:S(2)}) copy-start(bf16[240,1024]{1,0:T(8,128)(2,1)} %reshape.186) | copy-start | bytes 1474564
  256.2 10.4 %copy-start.13 = (bf16[240,768]{1,0:T(8,128)(2,1)S(1)}, bf16[240,768]{1,0:T(8,128)(2,1)}, u32[]{:S(2)}) copy-start(bf16[240,768]{1,0:T(8,128)(2,1)} %all-reduce.4.cloned.1.call-done) | copy-start | bytes 1105924
  256.2 10.4 %collective-permute-start.1 = (bf16[240,768]{1,0:T(8,128)(2,1)}, bf16[240,768]{1,0:T(8,128)(2,1)S(1)}, u32[]{:S(2)}, u32[]{:S(2)}) collective-permute-start(bf16[240,768]{1,0:T(8,128)(2,1)} %all-reduce.4.cloned.1.call-done), channel_id=1, source_target_pairs={{0,4},{4,0},{8,12},{12,8},{16,20},{20,16},{24,28},{28,24},{1,5},{5... | collective-permute-start | bytes 1105928 | tf_op jit(solution)/shard_map/ppermute | solution.py:16
Sparse Core Ops, SparseCore 0:
  82.5 40.4 all-reduce.5
  191.4 6.4 reduce-scatter.1
  231.9 24.2 all-reduce.3
where the time goes:
time: 279 us; the launch traced here: 277 us
  waiting for transfers between devices  114 us (41%)
  local copies, waits for them, and re-layouts  65.4 us (23%)
  starting transfers between devices  26.2 us (9%)
  matrix products  21.8 us (8%)
  other arithmetic  17.9 us (6%)
  blocking collectives  17.7 us (6%)
  between operations  14.1 us (5%)
    psum x1, waiting for transfers between devices, shards(): lax.psum(teach_stack.astype(jnp.bfloat16), 'group').astype(jnp.float32)  40.6 us
    psum x1, waiting for transfers between devices, shards(): lax.psum(back_hidden.astype(jnp.bfloat16), 'group').astype(jnp.float32)  24.4 us
    ppermute x2, waiting for transfers between devices, from_partner(): return lax.ppermute(block, axis, route)  22.5 us
    all_to_all x1, blocking collectives, shards(): lax.all_to_all(grad_send, 'expert', split_axis=0, concat_axis=0, tiled=True)  15.2 us
    dot_general x5, matrix products, across_width(): lax.dot_general(left_side, right_side, (((1,), (1,)), ((), ())), preferre...  10.2 us
    all_to_all x1, waiting for transfers between devices, shards(): lax.all_to_all(stud_part.astype(jnp.bfloat16).reshape(owners, 2 * capacit...  10.1 us
    slice x1, local copies, waits for them, and re-layouts, shards(): members[:, :, :, 0, :]  7.46 us
    all_to_all x1, waiting for transfers between devices, shards(): lax.all_to_all(stud_send, 'expert', split_axis=0, concat_axis=0, tiled=True)  7.32 us
  transfers between devices with their start and end apart: 9, of which 8 were waited for; matrix products, arithmetic and copies ran while one was open for 16% of the time, Pallas kernels for 0%

commit v1 on v0

--- a/solution.py
+++ b/solution.py
@@ -154,7 +154,9 @@
     back_hidden = across_width(column_piece, down_local)
     down_grad = inner_rows(stud_hidden, column_piece)
     back_hidden, down_grad = (back_hidden, down_grad)
-    back_hidden = lax.psum(back_hidden.astype(jnp.bfloat16), "group").astype(jnp.float32)
+    back_hidden = jnp.sum(lax.all_gather(back_hidden.astype(jnp.bfloat16), "group"), axis=0).astype(
+        jnp.float32
+    )
     back_hidden = back_hidden + from_partner(back_hidden.astype(jnp.bfloat16), "expert", 0).astype(
         back_hidden.dtype
     )

time: 279 us -> 265 us (0.950)
  waiting for transfers between devices: 114 us -> 88.9 us
  blocking collectives: 17.7 us -> 28.9 us
    psum x1 -> x0, waiting for transfers between devices: 24.4 us -> none  [shards(): lax.psum(back_hidden.astype(jnp.bfloat16), 'group').astype(jnp.float32)]
    all_gather x0 -> x1, blocking collectives: none -> 11.4 us  [shards(): lax.all_gather(back_hidden.astype(jnp.bfloat16), 'group')]
  transfers between devices with their start and end apart: 9 -> 8, of which waited for: 8 -> 7; matrix products, arithmetic and copies ran while one was open for 16% -> 17% of each run, Pallas kernels for 0% -> 0%
where the time goes in v1:
time: 265 us; the launch traced here: 263 us
  waiting for transfers between devices  88.9 us (34%)
  local copies, waits for them, and re-layouts  64.6 us (24%)
  blocking collectives  28.9 us (11%)
  starting transfers between devices  26.2 us (10%)
  matrix products  21.2 us (8%)
  other arithmetic  19.1 us (7%)
  between operations  14.4 us (5%)
    psum x1, waiting for transfers between devices, shards(): lax.psum(teach_stack.astype(jnp.bfloat16), 'group').astype(jnp.float32)  40.6 us
    ppermute x2, waiting for transfers between devices, from_partner(): return lax.ppermute(block, axis, route)  21.9 us
    all_to_all x1, blocking collectives, shards(): lax.all_to_all(grad_send, 'expert', split_axis=0, concat_axis=0, tiled=True)  15.2 us
    all_gather x1, blocking collectives, shards(): lax.all_gather(back_hidden.astype(jnp.bfloat16), 'group')  11.4 us
    all_to_all x1, waiting for transfers between devices, shards(): lax.all_to_all(stud_part.astype(jnp.bfloat16).reshape(owners, 2 * capacit...  10.1 us
    dot_general x5, matrix products, across_width(): lax.dot_general(left_side, right_side, (((1,), (1,)), ((), ())), preferre...  9.65 us
    slice x1, local copies, waits for them, and re-layouts, shards(): members[:, :, :, 0, :]  7.49 us
    all_to_all x1, waiting for transfers between devices, shards(): lax.all_to_all(stud_send, 'expert', split_axis=0, concat_axis=0, tiled=True)  7.32 us
  transfers between devices with their start and end apart: 8, of which 7 were waited for; matrix products, arithmetic and copies ran while one was open for 17% of the time, Pallas kernels for 0%

profile of v1, /device:TPU:0, one launch (start us, length us, event | category | flops | bytes accessed | tf_op | source)
XLA Modules:
  0.0 263.5 jit_solution(758478953875619845)
XLA Ops:
  7.2 0.9 broadcast_compare_fusion
  8.0 0.8 broadcast_multiply_fusion.1
  8.8 0.8 copy.50
  10.4 2.3 reduce-window.6
  13.3 6.2 %scatter_custom_fusion = s32[120]{0:T(128)S(1)} fusion(s32[1536]{0:T(1024)S(1)} %fusion.81, s32[1536]{0:T(1024)S(1)} %iota.27, s32[]{:T(128)} %constant.22.clone.1), kind=kCustom, calls=%fused_computation.115 | custom fusion | bytes 484 | tf_op jit(solution)/shard_map/scatter | solution.py:46
  19.5 3.4 %gather_fusion.1 = bf16[120,2048]{1,0:T(8,128)(2,1)} fusion(bf16[192,2048]{1,0:T(8,128)(2,1)} %param.10, s32[1024]{0:T(1024)S(1)} %get-tuple-element.11), kind=kCustom, calls=%fused_computation.1 | custom fusion | bytes 983520 | tf_op jit(solution)/shard_map/gather | solution.py:80
  22.9 2.0 gather.24
  25.0 1.9 broadcast_select_fusion
  26.9 7.3 %all-to-all-start.2 = ((bf16[8,15,2048]{2,1,0:T(8,128)(2,1)}), bf16[8,15,2048]{2,1,0:T(8,128)(2,1)}, u32[]{:S(2)}, u32[]{:S(2)}) async-start(bf16[8,15,2048]{2,1,0:T(8,128)(2,1)} %broadcast_select_fusion), calls=%async_computation.2 | async-start | bytes 1048576 | tf_op jit(solution)/shard_map/all_to_all | solution.py:88
  34.8 2.6 gather_fusion.2
  37.4 3.7 %reshape.185 = bf16[8,30,2,2,512]{4,3,2,1,0:T(2,128)(2,1)} reshape(bf16[16,15,2048]{2,1,0:T(8,128)(2,1)} %gather_fusion.2) | data formatting | bytes 1966080 | tf_op jit(solution)/shard_map/reshape | solution.py:83
  41.1 7.5 %slice_reduce_fusion.1 = (bf16[8,30,2,512]{3,2,1,0:T(2,128)(2,1)}, bf16[8,30,2,512]{3,2,1,0:T(2,128)(2,1)}) fusion(bf16[8,30,2,2,512]{4,3,2,1,0:T(2,128)(2,1)} %reshape.185), kind=kLoop, calls=%fused_computation.45 | loop fusion | bytes 1966080 | tf_op jit(solution)/shard_map/slice | solution.py:85
  48.6 2.1 reshape.274
  50.7 2.1 reshape.273
  52.8 1.7 copy_select_fusion
  54.6 1.1 copy.57
  55.6 6.0 %all-to-all-start = ((bf16[8,30,1024]{2,1,0:T(8,128)(2,1)}), bf16[8,30,1024]{2,1,0:T(8,128)(2,1)}, u32[]{:S(2)}, u32[]{:S(2)}) async-start(bf16[8,30,1024]{2,1,0:T(8,128)(2,1)} %copy.57), calls=%async_computation | async-start | bytes 1048576 | tf_op jit(solution)/shard_map/all_to_all | solution.py:89
  61.9 2.0 reshape.190
  63.8 3.3 %fusion.44 = bf16[1,120,768]{2,1,0:T(8,128)(2,1)S(1)} fusion(bf16[120,2048]{1,0:T(8,128)(2,1)} %reshape.190, bf16[1,768,2048]{2,1,0:T(8,128)(2,1)} %param.15), kind=kOutput, calls=%fused_computation.39 | convolution fusion | flops 377579520 | bytes 3821568 | tf_op jit(solution)/shard_map/dot_general | solution.py:24
  67.2 1.2 fusion.47
  68.4 7.3 %all-to-all-done = bf16[8,30,1024]{2,1,0:T(8,128)(2,1)} async-done(((bf16[8,30,1024]{2,1,0:T(8,128)(2,1)}), bf16[8,30,1024]{2,1,0:T(8,128)(2,1)}, u32[]{:S(2)}, u32[]{:S(2)}) %all-to-all-start) | async-done | bytes 491552 | tf_op jit(solution)/shard_map/all_to_all | solution.py:89
  75.7 2.0 reshape.186
  77.7 2.3 fusion.32
  80.7 0.8 pad_maximum_fusion.1
  81.4 0.9 pad_maximum_fusion
  82.4 40.6 %all-reduce.3.cloned.1.call-done = (bf16[2,120,768]{2,1,0:T(8,128)(2,1)}, bf16[2,240,768]{2,1,0:T(8,128)(2,1)}) async-done(((bf16[2,120,768]{2,1,0:T(8,128)(2,1)}, bf16[2,240,768]{2,1,0:T(8,128)(2,1)}), (bf16[2,120,768]{2,1,0:T(8,128)(2,1)}, bf16[2,240,768]{2,1,0:T(8,128)(2,1)})) %all-reduce.3.cloned.1.call-update) | async-done | bytes 1105936 | tf_op jit(solution)/shard_map/psum | solution.py:96
  123.0 1.5 collective-permute-start
  124.4 16.8 %collective-permute-done = bf16[2,240,768]{2,1,0:T(8,128)(2,1)S(1)} collective-permute-done((bf16[2,240,768]{2,1,0:T(8,128)(2,1)}, bf16[2,240,768]{2,1,0:T(8,128)(2,1)S(1)}, u32[]{:S(2)}, u32[]{:S(2)}) %collective-permute-start) | collective-permute-done | bytes 737312 | tf_op jit(solution)/shard_map/ppermute | solution.py:16
  141.2 1.3 convert_add_fusion
  142.5 1.1 copy-done.3
  143.6 1.4 fusion.20
  145.0 2.0 reshape.187
  147.0 5.5 %all-to-all-start.1 = ((bf16[8,30,1024]{2,1,0:T(8,128)(2,1)}), bf16[8,30,1024]{2,1,0:T(8,128)(2,1)}, u32[]{:S(2)}, u32[]{:S(2)}) async-start(bf16[8,30,1024]{2,1,0:T(8,128)(2,1)} %reshape.187), calls=%async_computation.1 | async-start | bytes 1048576 | tf_op jit(solution)/shard_map/all_to_all | solution.py:124
  152.6 1.4 fusion.6
  154.0 2.0 reshape.191
  156.0 10.1 %all-to-all-done.1 = bf16[8,30,1024]{2,1,0:T(8,128)(2,1)} async-done(((bf16[8,30,1024]{2,1,0:T(8,128)(2,1)}), bf16[8,30,1024]{2,1,0:T(8,128)(2,1)}, u32[]{:S(2)}, u32[]{:S(2)}) %all-to-all-start.1) | async-done | bytes 491552 | tf_op jit(solution)/shard_map/all_to_all | solution.py:124
  166.1 4.2 %all-to-all-start.3 = ((bf16[8,15,2048]{2,1,0:T(8,128)(2,1)}), bf16[8,15,2048]{2,1,0:T(8,128)(2,1)}, u32[]{:S(2)}, u32[]{:S(2)}) async-start(bf16[8,15,2048]{2,1,0:T(8,128)(2,1)} %reshape.191), calls=%async_computation.3 | async-start | bytes 1048576 | tf_op jit(solution)/shard_map/all_to_all | solution.py:117
  171.2 1.1 gather_fusion
  172.4 2.1 reshape.275
  174.5 2.2 copy.68
  176.6 2.1 reshape.276
  178.8 2.4 gather_fusion.3
  181.2 2.4 all-to-all-done.3
  183.6 2.3 convert_subtract_fusion
  185.9 2.3 sub.28
  188.2 1.3 broadcast_multiply_fusion
  189.5 1.7 convolution_convert_fusion.3
  191.4 6.5 %reduce-scatter.2.cloned.1.call-done = bf16[192,1,1024]{2,0,1:T(8,128)(2,1)} async-done(((bf16[192,2,1024]{2,0,1:T(8,128)(2,1)}), bf16[192,1,1024]{2,0,1:T(8,128)(2,1)}) %reduce-scatter.2.cloned.1.call-update) | async-done | bytes 393232 | tf_op jit(solution)/shard_map/reduce_scatter | solution.py:138
  197.9 2.0 bitcast_convert_fusion
  199.9 2.9 %gather_fusion.4 = f32[120,1024]{1,0:T(8,128)} fusion(f32[192,1024]{1,0:T(8,128)} %bitcast_convert_fusion, s32[1024]{0:T(1024)S(1)} %get-tuple-element.11), kind=kCustom, calls=%fused_computation.4 | custom fusion | bytes 983520 | tf_op jit(solution)/shard_map/gather | solution.py:145
  202.8 2.2 gather.28
  205.0 1.3 multiply_convert_fusion.1
  206.3 1.7 gather_fusion.5
  208.0 1.0 copy.69
  209.7 15.2 %all_to_all.25 = bf16[8,30,512]{2,1,0:T(8,128)(2,1)S(1)} all-to-all(bf16[8,30,512]{2,1,0:T(8,128)(2,1)} %reshape.277), channel_id=1, replica_groups=mesh['expert'=8,'replica'=2,'group'=2] {'expert'}, dimensions={0} | all-to-all | bytes 491520 | tf_op jit(solution)/shard_map/all_to_all | solution.py:149
  225.7 2.4 all_gather.9
  228.0 2.2 fusion.29
  230.2 11.4 %all-gather = bf16[480,768]{1,0:T(8,128)(2,1)} all-gather(bf16[240,768]{1,0:T(8,128)(2,1)S(1)} %fusion.29), channel_id=2, replica_groups=mesh['expert'=8,'replica'=2,'group'=2] {'group'}, dimensions={0}, use_global_device_ids=true | all-gather | bytes 1105920 | tf_op jit(solution)/shard_map/all_gather | solution.py:157
  241.6 1.3 reduce_sum.25
  242.9 1.5 collective-permute-start.1
  244.4 3.3 %fusion.19 = bf16[1,768,1024]{2,1,0:T(8,128)(2,1)} fusion(bf16[240,1024]{1,0:T(8,128)(2,1)} %copy-done.7, f32[2,240,768]{2,1,0:T(8,128)} %copy-done.3), kind=kOutput, calls=%fused_computation.28 | convolution fusion | flops 379379712 | bytes 3538944 | tf_op jit(solution)/shard_map/dot_general | solution.py:30
  247.7 5.1 %collective-permute-done.1 = bf16[240,768]{1,0:T(8,128)(2,1)S(1)} collective-permute-done((bf16[240,768]{1,0:T(8,128)(2,1)S(1)}, bf16[240,768]{1,0:T(8,128)(2,1)S(1)}, u32[]{:S(2)}, u32[]{:S(2)}) %collective-permute-start.1) | collective-permute-done | bytes 368672 | tf_op jit(solution)/shard_map/ppermute | solution.py:16
  252.8 2.0 fusion.17
  254.8 1.8 fusion.18
  (70 shorter events, 5.4 us)
Async XLA Ops:
  7.2 145.4 %copy-start = (bf16[1,768,2048]{2,1,0:T(8,128)(2,1)S(1)}, bf16[1,768,2048]{2,1,0:T(8,128)(2,1)}, u32[]{:S(2)}) copy-start(bf16[1,768,2048]{2,1,0:T(8,128)(2,1)} %param.16) | copy-start | bytes 9437188
  22.9 11.3 %copy-start.10 = (s32[8]{0:T(128)S(1)}, s32[8]{0:T(128)}, u32[]{:S(2)}) copy-start(s32[8]{0:T(128)} %param.13) | copy-start | bytes 100
  26.9 28.7 %all-to-all-start.2 = ((bf16[8,15,2048]{2,1,0:T(8,128)(2,1)}), bf16[8,15,2048]{2,1,0:T(8,128)(2,1)}, u32[]{:S(2)}, u32[]{:S(2)}) async-start(bf16[8,15,2048]{2,1,0:T(8,128)(2,1)} %broadcast_select_fusion), calls=%async_computation.2 | async-start | bytes 1048576 | tf_op jit(solution)/shard_map/all_to_all | solution.py:88
  55.6 20.1 %all-to-all-start = ((bf16[8,30,1024]{2,1,0:T(8,128)(2,1)}), bf16[8,30,1024]{2,1,0:T(8,128)(2,1)}, u32[]{:S(2)}, u32[]{:S(2)}) async-start(bf16[8,30,1024]{2,1,0:T(8,128)(2,1)} %copy.57), calls=%async_computation | async-start | bytes 1048576 | tf_op jit(solution)/shard_map/all_to_all | solution.py:89
  61.6 61.3 %all-reduce.3.cloned.1.call-start = ((), (), s32[]{:S(2)}) async-start(), calls=%async_computation.7 | async-start | bytes 2211840 | tf_op jit(solution)/shard_map/psum | solution.py:96
  63.8 3.4 %copy-start.1 = (bf16[120,2048]{1,0:T(8,128)(2,1)S(1)}, bf16[120,2048]{1,0:T(8,128)(2,1)}, u32[]{:S(2)}) copy-start(bf16[120,2048]{1,0:T(8,128)(2,1)} %reshape.190) | copy-start | bytes 1474564
  63.8 3.4 %copy-start.2 = (bf16[1,768,2048]{2,1,0:T(8,128)(2,1)S(1)}, bf16[1,768,2048]{2,1,0:T(8,128)(2,1)}, u32[]{:S(2)}) copy-start(bf16[1,768,2048]{2,1,0:T(8,128)(2,1)} %param.14) | copy-start | bytes 9437188
  77.7 2.3 copy-start.5
  77.7 2.3 copy-start.11
  123.0 20.7 %copy-start.12 = (bf16[1,768,1024]{2,1,0:T(8,128)(2,1)S(1)}, bf16[1,768,1024]{2,1,0:T(8,128)(2,1)}, u32[]{:S(2)}) copy-start(bf16[1,768,1024]{2,1,0:T(8,128)(2,1)} %param.19) | copy-start | bytes 4718596
  123.0 18.3 %collective-permute-start = (bf16[2,240,768]{2,1,0:T(8,128)(2,1)}, bf16[2,240,768]{2,1,0:T(8,128)(2,1)S(1)}, u32[]{:S(2)}, u32[]{:S(2)}) collective-permute-start(bf16[2,240,768]{2,1,0:T(8,128)(2,1)} %get-tuple-element.7), channel_id=1, source_target_pairs={{0,4},{4,0},{8,12},{12,8},{16,20},{20,16},{24,28},{28,24},{1,5},{5... | collective-permute-start | bytes 2211848 | tf_op jit(solution)/shard_map/ppermute | solution.py:16
  142.5 1.1 copy-start.3
  145.0 7.5 %copy-start.8 = (bf16[2,120,768]{2,1,0:T(8,128)(2,1)S(1)}, bf16[2,120,768]{2,1,0:T(8,128)(2,1)}, u32[]{:S(2)}) copy-start(bf16[2,120,768]{2,1,0:T(8,128)(2,1)} %get-tuple-element.6) | copy-start | bytes 1105924
  147.0 19.1 %all-to-all-start.1 = ((bf16[8,30,1024]{2,1,0:T(8,128)(2,1)}), bf16[8,30,1024]{2,1,0:T(8,128)(2,1)}, u32[]{:S(2)}, u32[]{:S(2)}) async-start(bf16[8,30,1024]{2,1,0:T(8,128)(2,1)} %reshape.187), calls=%async_computation.1 | async-start | bytes 1048576 | tf_op jit(solution)/shard_map/all_to_all | solution.py:124
  154.0 16.3 %copy-start.9 = (f32[192,8]{0,1:T(8,128)S(1)}, f32[192,8]{0,1:T(8,128)}, u32[]{:S(2)}) copy-start(f32[192,8]{0,1:T(8,128)} %param.12) | copy-start | bytes 18436
  166.1 17.5 %all-to-all-start.3 = ((bf16[8,15,2048]{2,1,0:T(8,128)(2,1)}), bf16[8,15,2048]{2,1,0:T(8,128)(2,1)}, u32[]{:S(2)}, u32[]{:S(2)}) async-start(bf16[8,15,2048]{2,1,0:T(8,128)(2,1)} %reshape.191), calls=%async_computation.3 | async-start | bytes 1048576 | tf_op jit(solution)/shard_map/all_to_all | solution.py:117
  170.3 27.6 %reduce-scatter.2.cloned.1.call-start = ((), (), s32[]{:S(2)}) async-start(), calls=%async_computation.6 | async-start | bytes 1179648 | tf_op jit(solution)/shard_map/reduce_scatter | solution.py:138
  228.0 13.6 %copy-start.7 = (bf16[240,1024]{1,0:T(8,128)(2,1)}, bf16[240,1024]{1,0:T(8,128)(2,1)S(1)}, u32[]{:S(2)}) copy-start(bf16[240,1024]{1,0:T(8,128)(2,1)S(1)} %all_gather.9) | copy-start | bytes 1474564
  242.9 9.9 %copy-start.4 = (f32[2,240,768]{2,1,0:T(8,128)S(1)}, f32[2,240,768]{2,1,0:T(8,128)}, u32[]{:S(2)}) copy-start(f32[2,240,768]{2,1,0:T(8,128)} %copy-done.3) | copy-start | bytes 4423684
  242.9 9.8 %copy-start.6 = (bf16[240,1024]{1,0:T(8,128)(2,1)S(1)}, bf16[240,1024]{1,0:T(8,128)(2,1)}, u32[]{:S(2)}) copy-start(bf16[240,1024]{1,0:T(8,128)(2,1)} %reshape.186) | copy-start | bytes 1474564
  242.9 9.8 %collective-permute-start.1 = (bf16[240,768]{1,0:T(8,128)(2,1)S(1)}, bf16[240,768]{1,0:T(8,128)(2,1)S(1)}, u32[]{:S(2)}, u32[]{:S(2)}) collective-permute-start(bf16[240,768]{1,0:T(8,128)(2,1)S(1)} %reduce_sum.25), channel_id=1, source_target_pairs={{0,4},{4,0},{8,12},{12,8},{16,20},{20,16},{24,28},{28,24},{1,5},{5... | collective-permute-start | bytes 1105928 | tf_op jit(solution)/shard_map/ppermute | solution.py:16
Sparse Core Ops, SparseCore 0:
  82.5 40.4 all-reduce.2
  191.4 6.4 reduce-scatter.1
